TPU v7x, 32 devices: a whole 2x2x4 slice. The times are simulated.
32 devices in a mesh: gx: 4 (over x, core), gy: 4 (over z), gz: 2 (over y).
Axes of the slice: x: 2, y: 2, z: 4, core: 2. Of those that a mesh axis runs over, the one named last changes fastest.
Arguments:
- layer_input: bfloat16 [1024, 4096], P('gz', ('gx', 'gy')), may hold values from -6 to 6
- modality: int32 [1024], P('gz'), may hold values 0 or 1
- image_spans: int32 [2, 8], replicated, may hold values from 0 to 1024, as said below
- norm_gain: float32 [2, 4096], P(None, ('gx', 'gy')), may hold values from 0.1 to 1.9
- w_qkv: bfloat16 [3, 4096, 2048], P(None, 'gz', ('gx', 'gy')), as said below
- w_out: bfloat16 [2048, 4096], P(('gx', 'gy'), 'gz'), may hold values from -0.125 to 0.125
- grad_out: bfloat16 [1024, 4096], P('gz', ('gx', 'gy')), may hold values from -6 to 6
Outputs:
- attn_out: bfloat16 [1024, 4096], P('gz', ('gx', 'gy'))
- grad_in: bfloat16 [1024, 4096], P('gz', ('gx', 'gy'))
- grad_qkv: float32 [3, 4096, 2048], P(None, 'gz', ('gx', 'gy'))
- grad_wout: float32 [2048, 4096], P(('gx', 'gy'), 'gz')
- grad_gain: float32 [2, 4096], P(None, ('gx', 'gy'))
Inputs may be any that keep to these rules, and one draw needn't show every extreme that they name: `image_spans`: row 0 holds the first position of each of 8 image spans, in increasing order, and row 1 one past its last; spans are disjoint and none is empty. `w_qkv`: entries are at most 20 * 4096 ** -0.5 in magnitude.
All inputs are finite; a program needn't handle non-finite values. No bound on the sum of `modality` on one device may be relied on, other than what follows from the above.
Results may differ from a plain program's by a relative error of at most 0.035.
The roundings to bfloat16 on the way count: a program that leaves them out, or rounds other values in their place, can miss the bound.
Values may be sent and summed in bfloat16 or wider, within the bound.
A program may use at most 128 MiB of HBM per device.

v0:
```python
import math
import jax
import jax.numpy as jnp
from jax import lax
from jax.sharding import PartitionSpec as P

epsilon = 1e-05
masked_low = -1e30


def span_index(positions, image_spans):
    inside = (positions[:, None] >= image_spans[0][None, :]) & (
        positions[:, None] < image_spans[1][None, :]
    )
    labels = jnp.arange(1, image_spans.shape[1] + 1, dtype=jnp.int32)
    return jnp.sum(jnp.where(inside, labels[None, :], 0), axis=1) - 1


def visible(query_pos, query_span, key_pos, key_span):
    causal = key_pos[None, :] <= query_pos[:, None]
    same_image = (query_span[:, None] == key_span[None, :]) & (query_span[:, None] >= 0)
    return causal | same_image


def per_device(layer_input, modality, image_spans, norm_gain, w_qkv, w_out, grad_out):
    tok_rows, local_width = layer_input.shape
    full_width = local_width * lax.axis_size(("gx", "gy"))
    head_dim = w_qkv.shape[2]
    inputs_f = layer_input.astype(jnp.float32)
    squares = lax.psum(jnp.sum(inputs_f * inputs_f, axis=1), ("gx", "gy"))
    inv_rms = lax.rsqrt(squares / full_width + epsilon)
    row_gain = jnp.where(modality[:, None] == 1, norm_gain[1][None, :], norm_gain[0][None, :])
    scaled = inputs_f * inv_rms[:, None]
    normed = (scaled * row_gain).astype(jnp.bfloat16)
    w_full = lax.all_gather(w_qkv, "gz", axis=1, tiled=True)
    wo_full = lax.all_gather(w_out, "gz", axis=1, tiled=True)
    rows_block = w_full
    projected = jnp.einsum(
        "tc,mch->mth",
        lax.all_gather(normed, ("gx", "gy"), axis=1, tiled=True),
        rows_block,
        preferred_element_type=jnp.float32,
    )
    projected = projected.astype(jnp.bfloat16)
    queries = projected[0]
    keys_values = lax.all_gather(
        jnp.concatenate([projected[1], projected[2]], axis=1), "gz", axis=0, tiled=True
    )
    key_total = keys_values.shape[0]
    query_pos = lax.axis_index("gz") * tok_rows + jnp.arange(tok_rows, dtype=jnp.int32)
    query_span = span_index(query_pos, image_spans)
    key_block = 512
    block_count = key_total // key_block
    score_scale = 1.0 / math.sqrt(head_dim)
    block_ids = jnp.arange(block_count, dtype=jnp.int32)

    def block_scores(block_idx):
        first_key = block_idx * key_block
        kv_block = lax.dynamic_slice_in_dim(keys_values, first_key, key_block, 0)
        key_pos = first_key + jnp.arange(key_block, dtype=jnp.int32)
        allowed = visible(query_pos, query_span, key_pos, span_index(key_pos, image_spans))
        scores = (
            lax.dot_general(
                queries,
                kv_block[:, :head_dim],
                (((1,), (1,)), ((), ())),
                preferred_element_type=jnp.float32,
            )
            * score_scale
        )
        return (kv_block, allowed, scores)

    def gather_stats(state, block_idx):
        maxima, summed = state
        kv_block, allowed, scores = block_scores(block_idx)
        new_maxima = jnp.maximum(maxima, jnp.max(jnp.where(allowed, scores, masked_low), axis=1))
        fresh = jnp.sum(jnp.where(allowed, jnp.exp(scores - new_maxima[:, None]), 0.0), axis=1)
        return ((new_maxima, summed * jnp.exp(maxima - new_maxima) + fresh), None)

    start_state = (
        jnp.full((tok_rows,), masked_low, jnp.float32),
        jnp.zeros((tok_rows,), jnp.float32),
    )
    (maxima, summed), unused = lax.scan(gather_stats, start_state, block_ids)
    lse = maxima + jnp.log(summed)

    def block_probs(block_idx):
        kv_block, allowed, scores = block_scores(block_idx)
        return (kv_block, jnp.where(allowed, jnp.exp(scores - lse[:, None]), 0.0))

    def attend(accum, block_idx):
        kv_block, attn_p = block_probs(block_idx)
        return (
            accum
            + jnp.dot(
                attn_p.astype(jnp.bfloat16),
                kv_block[:, head_dim:],
                preferred_element_type=jnp.float32,
            ),
            None,
        )

    attended_f, unused = lax.scan(attend, jnp.zeros((tok_rows, head_dim), jnp.float32), block_ids)
    attended = attended_f.astype(jnp.bfloat16)
    all_heads = lax.all_gather(attended, ("gx", "gy"), axis=1, tiled=True)
    out_rows = lax.all_to_all(wo_full, ("gx", "gy"), split_axis=1, concat_axis=0, tiled=True)
    head_total = out_rows.shape[0] // head_dim
    per_head = jnp.einsum(
        "thd,hdc->htc",
        all_heads.reshape(tok_rows, head_total, head_dim),
        out_rows.reshape(head_total, head_dim, local_width),
        preferred_element_type=jnp.float32,
    )
    per_head = lax.optimization_barrier(per_head.astype(jnp.bfloat16)).astype(jnp.float32)
    attn_out = jnp.sum(per_head, axis=0).astype(jnp.bfloat16)
    segment = lax.all_gather(grad_out, ("gx", "gy"), axis=1, tiled=True)
    d_accum = lax.dot_general(
        segment, wo_full, (((1,), (1,)), ((), ())), preferred_element_type=jnp.float32
    )
    partial_value = lax.dot_general(
        attended, segment, (((0,), (0,)), ((), ())), preferred_element_type=jnp.float32
    )
    d_attended = d_accum.astype(jnp.bfloat16)
    row_dots = jnp.sum(d_attended.astype(jnp.float32) * attended.astype(jnp.float32), axis=1)

    def backward_block(d_query, block_idx):
        kv_block, attn_p = block_probs(block_idx)
        d_probs = lax.dot_general(
            d_attended,
            kv_block[:, head_dim:],
            (((1,), (1,)), ((), ())),
            preferred_element_type=jnp.float32,
        )
        d_scores = (attn_p * (d_probs - row_dots[:, None]) * score_scale).astype(jnp.bfloat16)
        d_query = d_query + jnp.dot(
            d_scores, kv_block[:, :head_dim], preferred_element_type=jnp.float32
        )
        d_keys = lax.dot_general(
            d_scores, queries, (((0,), (0,)), ((), ())), preferred_element_type=jnp.float32
        )
        d_values = lax.dot_general(
            attn_p.astype(jnp.bfloat16),
            d_attended,
            (((0,), (0,)), ((), ())),
            preferred_element_type=jnp.float32,
        )
        return (d_query, jnp.concatenate([d_keys, d_values], axis=1))

    d_query_f, kv_parts = lax.scan(
        backward_block, jnp.zeros((tok_rows, head_dim), jnp.float32), block_ids
    )
    kv_grad = lax.psum_scatter(
        kv_parts.reshape(key_total, 2 * head_dim).astype(jnp.bfloat16),
        "gz",
        scatter_dimension=0,
        tiled=True,
    ).astype(jnp.float32)
    grads = jnp.stack(
        [
            d_query_f.astype(jnp.bfloat16),
            kv_grad[:, :head_dim].astype(jnp.bfloat16),
            kv_grad[:, head_dim:].astype(jnp.bfloat16),
        ]
    )
    w_grad = jnp.einsum(
        "tc,mth->mch",
        lax.all_gather(normed, ("gx", "gy"), axis=1, tiled=True),
        grads,
        preferred_element_type=jnp.float32,
    )
    grad_qkv, grad_wout = (
        lax.psum_scatter(w_grad.astype(jnp.bfloat16), "gz", scatter_dimension=1, tiled=True).astype(
            jnp.float32
        ),
        lax.psum_scatter(
            partial_value.astype(jnp.bfloat16), "gz", scatter_dimension=1, tiled=True
        ).astype(jnp.float32),
    )
    rows_block = w_full
    grad_normed = (
        lax.psum_scatter(
            jnp.einsum("mch,mth->ct", rows_block, grads, preferred_element_type=jnp.float32).astype(
                jnp.bfloat16
            ),
            ("gx", "gy"),
            scatter_dimension=0,
            tiled=True,
        )
        .astype(jnp.float32)
        .T
    )
    upstream = grad_normed * row_gain
    norm_dots = lax.psum(jnp.sum(upstream * scaled, axis=1), ("gx", "gy"))
    grad_in = (inv_rms[:, None] * (upstream - scaled * (norm_dots / full_width)[:, None])).astype(
        jnp.bfloat16
    )
    onehot = (modality[:, None] == jnp.arange(2, dtype=jnp.int32)[None, :]).astype(jnp.float32)
    local_gain = jnp.dot(onehot.T, grad_normed * scaled, precision=lax.Precision.HIGHEST)
    grad_gain = lax.psum(local_gain, "gz")
    return (attn_out, grad_in, grad_qkv, grad_wout, grad_gain)


def solution(mesh):
    in_specs = (
        P("gz", ("gx", "gy")),
        P("gz"),
        P(),
        P(None, ("gx", "gy")),
        P(None, "gz", ("gx", "gy")),
        P(("gx", "gy"), "gz"),
        P("gz", ("gx", "gy")),
    )
    out_specs = (
        P("gz", ("gx", "gy")),
        P("gz", ("gx", "gy")),
        P(None, "gz", ("gx", "gy")),
        P(("gx", "gy"), "gz"),
        P(None, ("gx", "gy")),
    )
    return jax.shard_map(
        per_device, mesh=mesh, in_specs=in_specs, out_specs=out_specs, check_vma=False
    )
```

profile of v0, /device:TPU:0, one launch (start us, length us, event | category | flops | bytes accessed | tf_op | source)
XLA Modules:
  0.0 420.7 jit_solution(4267195177550142330)
XLA Ops:
  7.3 2.7 copy.44
  10.2 35.2 %psum.21 = f32[512]{0:T(512)S(1)} all-reduce(f32[512]{0:T(512)S(1)} %fusion.65), channel_id=1, replica_groups=mesh['gx'=4,'gy'=4,'gz'=2] {'gx','gy'}, use_global_device_ids=true, to_apply=%region_1.0 | all-reduce | flops 512 | bytes 4096 | tf_op jit(solution)/shard_map/psum | solution.py:30
  45.4 0.9 fusion.66
  46.4 1.0 copy.50
  47.5 0.5 all-gather.14.cloned.1.call-update
  48.3 9.5 %all-gather.8.cloned.1.call-done = bf16[3,4096,128]{1,2,0:T(8,128)(2,1)} async-done(((bf16[3,2048,128]{1,2,0:T(8,128)(2,1)}), bf16[3,4096,128]{1,2,0:T(8,128)(2,1)}) %all-gather.8.cloned.1.call-update) | async-done | bytes 3145744 | tf_op jit(solution)/shard_map/all_gather | solution.py:35
  57.8 55.2 %all-gather.6.cloned.1.call-done = bf16[512,4096]{1,0:T(8,128)(2,1)} async-done(((bf16[512,256]{1,0:T(8,128)(2,1)}), bf16[512,4096]{1,0:T(8,128)(2,1)}) %all-gather.6.cloned.1.call-update) | async-done | bytes 4194320 | tf_op jit(solution)/shard_map/all_gather | solution.py:40
  113.0 5.0 %fusion.75 = f32[512,384]{0,1:S(1)} fusion(bf16[512,4096]{1,0:T(8,128)(2,1)} %all-gather.6.cloned.1.call-done, bf16[4096,384]{0,1:T(8,128)(2,1)} %bitcast.156), kind=kOutput, calls=%fused_computation.134 | convolution fusion | flops 1610612736 | bytes 8126464
  118.1 13.9 %all_gather.21 = bf16[1024,256]{0,1:T(8,128)(2,1)S(1)} all-gather(bf16[512,256]{0,1:T(8,128)(2,1)S(1)} %pad_maximum_fusion.1), channel_id=1, replica_groups=mesh['gx'=4,'gy'=4,'gz'=2] {'gz'}, dimensions={0}, use_global_device_ids=true | all-gather | bytes 786432 | tf_op jit(solution)/shard_map/all_gather | solution.py:46
  132.4 4.8 %while.43 = (s32[]{:T(128)}, f32[512]{0:T(512)S(1)}, f32[512]{0:T(512)S(1)}, s32[2]{0:T(128)S(1)}, s32[512]{0:T(512)S(1)}, /*index=5*/s32[2,8]{1,0:T(2,128)S(1)}...) while((s32[]{:T(128)}, f32[512]{0:T(512)S(1)}, ...), condition=%wide.region_7.8_spmd.clone, body=%wide.region_3.7_spmd.clone.sunk | while | flops 70803472 | bytes 2418638 | solution.py:84
  132.4 0.6 dynamic_slice.46
  134.8 0.6 dynamic_slice.46
  137.2 0.6 log_add_fusion
  137.7 5.9 %while.44 = (s32[]{:T(128)}, f32[512,128]{1,0:T(8,128)S(1)}, s32[2]{0:T(128)S(1)}, s32[512]{0:T(512)S(1)}, s32[2,8]{1,0:T(2,128)S(1)}, /*index=5*/bf16[1024,256]...) while((s32[]{:T(128)}, f32[512,128]{1,0:T(8,128)S(1)}, ...), condition=%wide.region_10.11_spmd.clone, body=%wide.region_8.10_spmd.clone.sunk | while | flops 136467984 | bytes 945628 | solution.py:103
  137.7 0.6 dynamic_slice.47
  139.1 1.5 fusion.118
  140.7 0.6 dynamic_slice.47
  142.1 1.5 fusion.118
  143.8 47.6 %all-gather.14.cloned.1.call-done = bf16[512,4096]{1,0:T(8,128)(2,1)} async-done(((bf16[512,256]{1,0:T(8,128)(2,1)}), bf16[512,4096]{1,0:T(8,128)(2,1)}) %all-gather.14.cloned.1.call-update) | async-done | bytes 4194320 | tf_op jit(solution)/shard_map/all_gather | solution.py:116
  191.3 4.0 multiply_reduce_fusion
  196.0 9.3 %while.45 = (s32[]{:T(128)}, f32[512,128]{1,0:T(8,128)S(1)}, bf16[2,512,256]{1,2,0:T(8,128)(2,1)S(1)}, s32[2]{0:T(128)}, s32[512]{0:T(512)S(1)}, /*index=5*/s32[...) while((s32[]{:T(128)}, f32[512,128]{1,0:T(8,128)S(1)}, ...), condition=%wide.region_15.16_spmd.clone, body=%wide.region_13.15_spmd.clone.sunk | while | flops 339367424 | bytes 6974985 | solution.py:149
  196.0 1.2 dynamic_slice.48
  198.0 1.2 fusion.129
  200.6 1.2 dynamic_slice.48
  202.7 1.2 fusion.129
  205.3 1.0 copy.56
  206.4 3.9 convolution_convert_fusion.1
  210.3 0.7 all-gather.10.cloned.1.call-update
  211.1 8.2 %reduce-scatter.5.cloned.1.call-done = bf16[512,256]{1,0:T(8,128)(2,1)} async-done(((bf16[1024,256]{1,0:T(8,128)(2,1)}), bf16[512,256]{1,0:T(8,128)(2,1)}) %reduce-scatter.5.cloned.1.call-update) | async-done | bytes 262160 | tf_op jit(solution)/shard_map/reduce_scatter | solution.py:152
  219.2 1.0 slice_bitcast_fusion.7
  220.2 5.8 %fusion.52 = bf16[4096,512]{0,1:T(8,128)(2,1)} fusion(bf16[3,4096,128]{1,2,0:T(8,128)(2,1)} %all-gather.8.cloned.1.call-done, bf16[1,512,128]{2,1,0:T(8,128)(2,1)S(1)} %get-tuple-element.678, bf16[1,512,128]{2,1,0:T(8,128)(2,1)S(1)} %get-tuple-element.677, bf16[1,512,128]{2,1,0:T(8,128)(2,1)S(1)} %convert_bitcast_fusion.1), kind=kOutput, calls=%fused_computation.84 | convolution fusion | flops 1613103104 | bytes 7733248 | tf_op jit(solution)/shard_map/mch,mth->ct/dot_general | solution.py:182
  226.3 6.1 %fusion.53 = bf16[3,4096,128]{1,2,0:T(8,128)(2,1)} fusion(bf16[512,4096]{1,0:T(8,128)(2,1)} %all-gather.6.cloned.1.call-done, bf16[1,512,128]{2,1,0:T(8,128)(2,1)S(1)} %get-tuple-element.678, bf16[1,512,128]{2,1,0:T(8,128)(2,1)S(1)} %get-tuple-element.677, bf16[1,512,128]{2,1,0:T(8,128)(2,1)S(1)} %convert_bitcast_fusion.1), kind=kOutput, calls=%fused_computation.85 | convolution fusion | flops 1612578816 | bytes 7733248 | tf_op jit(solution)/shard_map/tc,mth->mch/dot_general | solution.py:165
  232.4 1.3 copy.51
  233.8 5.5 %all-to-all-start = ((bf16[128,16,256]{2,0,1:T(8,128)(2,1)}), bf16[128,16,256]{2,0,1:T(8,128)(2,1)S(1)}, u32[]{:S(2)}, u32[]{:S(2)}) async-start(bf16[128,16,256]{2,0,1:T(8,128)(2,1)} %copy.51), calls=%async_computation | async-start | bytes 2097152 | tf_op jit(solution)/shard_map/all_to_all | solution.py:106
  239.3 3.1 reduce-scatter.11.cloned.1.call-done
  242.4 2.1 convert_element_type.104
  244.5 25.8 %all-to-all-done = bf16[128,16,256]{2,0,1:T(8,128)(2,1)S(1)} async-done(((bf16[128,16,256]{2,0,1:T(8,128)(2,1)}), bf16[128,16,256]{2,0,1:T(8,128)(2,1)S(1)}, u32[]{:S(2)}, u32[]{:S(2)}) %all-to-all-start) | async-done | bytes 1048608 | tf_op jit(solution)/shard_map/all_to_all | solution.py:106
  270.3 19.1 %all-gather.10.cloned.1.call-done = bf16[512,2048]{0,1:T(8,128)(2,1)} async-done(((bf16[512,128]{0,1:T(8,128)(2,1)}), bf16[512,2048]{0,1:T(8,128)(2,1)}) %all-gather.10.cloned.1.call-update) | async-done | bytes 2097168 | tf_op jit(solution)/shard_map/all_gather | solution.py:105
  289.4 4.8 %convolution_convert_fusion.2 = bf16[16,512,256]{2,1,0:T(8,128)(2,1)} fusion(bf16[512,16,128]{0,2,1:T(8,128)(2,1)} %bitcast.147, bf16[128,16,256]{2,0,1:T(8,128)(2,1)S(1)} %all-to-all-done), kind=kOutput, calls=%fused_computation.88 | convolution fusion | flops 538968064 | bytes 7340032 | tf_op jit(solution)/shard_map/thd,hdc->htc/dot_general | solution.py:108
  294.2 3.5 reduce_sum.98
  297.8 67.0 %reduce-scatter.7.cloned.1.call-done = bf16[256,512]{0,1:T(8,128)(2,1)} async-done(((bf16[4096,512]{0,1:T(8,128)(2,1)}), bf16[256,512]{0,1:T(8,128)(2,1)}) %reduce-scatter.7.cloned.1.call-update) | async-done | bytes 262160 | tf_op jit(solution)/shard_map/reduce_scatter | solution.py:181
  364.8 1.3 fusion.59
  366.1 30.5 %psum.22 = f32[512]{0:T(512)S(1)} all-reduce(f32[512]{0:T(512)S(1)} %fusion.59), channel_id=1, replica_groups=mesh['gx'=4,'gy'=4,'gz'=2] {'gx','gy'}, use_global_device_ids=true, to_apply=%region_19.20 | all-reduce | flops 512 | bytes 4096 | tf_op jit(solution)/shard_map/psum | solution.py:193
  396.6 1.5 fusion.63
  398.1 5.7 %psum.23 = f32[2,256]{1,0:T(2,128)} all-reduce(f32[2,256]{1,0:T(2,128)S(1)} %fusion.63), channel_id=1, replica_groups=mesh['gx'=4,'gy'=4,'gz'=2] {'gz'}, use_global_device_ids=true, to_apply=%region_22.23 | all-reduce | flops 512 | bytes 4096 | tf_op jit(solution)/shard_map/psum | solution.py:199
  403.8 6.4 %reduce-scatter.9.cloned.1.call-done = bf16[3,2048,128]{1,2,0:T(8,128)(2,1)} async-done(((bf16[3,4096,128]{1,2,0:T(8,128)(2,1)}), bf16[3,2048,128]{1,2,0:T(8,128)(2,1)}) %reduce-scatter.9.cloned.1.call-update) | async-done | bytes 1572880 | tf_op jit(solution)/shard_map/reduce_scatter | solution.py:172
  410.2 3.1 copy.59
  413.2 1.0 fusion.62
  (129 shorter events, 7.5 us)
Async XLA Ops:
  7.2 2.8 copy-start
  7.2 38.2 %copy-start.12 = (s32[512]{0:T(512)S(1)}, s32[512]{0:T(512)}, u32[]{:S(2)}) copy-start(s32[512]{0:T(512)} %param.14) | copy-start | bytes 6148
  7.2 38.2 %copy-start.14 = (f32[2,256]{1,0:T(2,128)S(1)}, f32[2,256]{1,0:T(2,128)}, u32[]{:S(2)}) copy-start(f32[2,256]{1,0:T(2,128)} %param.16) | copy-start | bytes 6148
  7.2 39.2 %copy-start.4 = (bf16[128,2048]{1,0:T(8,128)(2,1)S(1)}, bf16[128,2048]{1,0:T(8,128)(2,1)}, u32[]{:S(2)}) copy-start(bf16[128,2048]{1,0:T(8,128)(2,1)} %param.18) | copy-start | bytes 1572868
  7.2 41.0 %copy-start.5 = (s32[2,8]{1,0:T(2,128)S(1)}, s32[2,8]{1,0:T(2,128)}, u32[]{:S(2)}) copy-start(s32[2,8]{1,0:T(2,128)} %param.15) | copy-start | bytes 196
  7.2 50.6 %all-gather.8.cloned.1.call-start = ((), (), s32[]{:S(2)}) async-start(), calls=%async_computation.6 | async-start | bytes 4718592 | tf_op jit(solution)/shard_map/all_gather | solution.py:35
  10.0 103.0 %all-gather.6.cloned.1.call-start = ((), (), s32[]{:S(2)}) async-start(), calls=%async_computation.5 | async-start | bytes 4456448 | tf_op jit(solution)/shard_map/all_gather | solution.py:40
  45.4 2.8 copy-start.10
  45.4 2.7 copy-start.8
  45.4 72.6 %copy-start.6 = (f32[1,256]{1,0:T(1,128)}, f32[1,256]{1,0:T(1,128)S(1)}, u32[]{:S(2)}) copy-start(f32[1,256]{1,0:T(1,128)S(1)} %get-tuple-element.679) | copy-start | bytes 3076
  46.3 97.4 %all-gather.12.cloned.1.call-start = ((), (), s32[]{:S(2)}) async-start(), calls=%async_computation.8 | async-start | bytes 1572864 | tf_op jit(solution)/shard_map/all_gather | solution.py:36
  47.4 143.9 %all-gather.14.cloned.1.call-start = ((), (), s32[]{:S(2)}) async-start(), calls=%async_computation.9 | async-start | bytes 4456448 | tf_op jit(solution)/shard_map/all_gather | solution.py:116
  48.0 171.2 %reduce-scatter.5.cloned.1.call-start = ((), (), s32[]{:S(2)}) async-start(), calls=%async_computation.10 | async-start | bytes 786432 | tf_op jit(solution)/shard_map/reduce_scatter | solution.py:152
  143.7 62.6 %copy-start.2 = (bf16[512,128]{0,1:T(8,128)(2,1)}, bf16[512,128]{0,1:T(8,128)(2,1)S(1)}, u32[]{:S(2)}) copy-start(bf16[512,128]{0,1:T(8,128)(2,1)S(1)} %copy.49) | copy-start | bytes 393220
  206.3 36.1 %reduce-scatter.11.cloned.1.call-start = ((), (), s32[]{:S(2)}) async-start(), calls=%async_computation.13 | async-start | bytes 1572864 | tf_op jit(solution)/shard_map/reduce_scatter | solution.py:175
  210.3 79.1 %all-gather.10.cloned.1.call-start = ((), (), s32[]{:S(2)}) async-start(), calls=%async_computation.7 | async-start | bytes 2228224 | tf_op jit(solution)/shard_map/all_gather | solution.py:105
  211.0 153.8 %reduce-scatter.7.cloned.1.call-start = ((), (), s32[]{:S(2)}) async-start(), calls=%async_computation.11 | async-start | bytes 4456448 | tf_op jit(solution)/shard_map/reduce_scatter | solution.py:181
  226.1 6.4 %copy-start.1 = (bf16[128,4096]{0,1:T(8,128)(2,1)S(1)}, bf16[128,4096]{0,1:T(8,128)(2,1)}, u32[]{:S(2)}) copy-start(bf16[128,4096]{0,1:T(8,128)(2,1)} %all-gather.12.cloned.1.call-done) | copy-start | bytes 3145732
  226.1 184.1 %reduce-scatter.9.cloned.1.call-start = ((), (), s32[]{:S(2)}) async-start(), calls=%async_computation.12 | async-start | bytes 4718592 | tf_op jit(solution)/shard_map/reduce_scatter | solution.py:172
  233.8 36.5 %all-to-all-start = ((bf16[128,16,256]{2,0,1:T(8,128)(2,1)}), bf16[128,16,256]{2,0,1:T(8,128)(2,1)S(1)}, u32[]{:S(2)}, u32[]{:S(2)}) async-start(bf16[128,16,256]{2,0,1:T(8,128)(2,1)} %copy.51), calls=%async_computation | async-start | bytes 2097152 | tf_op jit(solution)/shard_map/all_to_all | solution.py:106
  289.4 75.4 %copy-start.7 = (f32[1,256]{1,0:T(1,128)S(1)}, f32[1,256]{1,0:T(1,128)}, u32[]{:S(2)}) copy-start(f32[1,256]{1,0:T(1,128)} %copy-done.6) | copy-start | bytes 3076
  289.4 75.4 %copy-start.9 = (f32[1,256]{1,0:T(1,128)S(1)}, f32[1,256]{1,0:T(1,128)}, u32[]{:S(2)}) copy-start(f32[1,256]{1,0:T(1,128)} %copy-done.8) | copy-start | bytes 3076
  289.4 75.4 %copy-start.11 = (pred[512]{0:T(512)(128)(4,1)S(1)}, pred[512]{0:T(512)(128)(4,1)}, u32[]{:S(2)}) copy-start(pred[512]{0:T(512)(128)(4,1)} %copy-done.10) | copy-start | bytes 1540
  294.2 102.4 %copy-start.13 = (s32[512]{0:T(512)S(1)}, s32[512]{0:T(512)}, u32[]{:S(2)}) copy-start(s32[512]{0:T(512)} %param.14) | copy-start | bytes 6148
  364.8 48.5 %copy-start.3 = (bf16[256,512]{0,1:T(8,128)(2,1)S(1)}, bf16[256,512]{0,1:T(8,128)(2,1)}, u32[]{:S(2)}) copy-start(bf16[256,512]{0,1:T(8,128)(2,1)} %reduce-scatter.7.cloned.1.call-done) | copy-start | bytes 786436
Sparse Core Ops, SparseCore 0:
  10.1 47.6 all-gather.7
  60.5 52.4 all-gather.5
  115.1 23.5 all-gather.11
  140.6 50.6 all-gather.13
  206.4 12.7 reduce-scatter.4
  221.9 20.3 reduce-scatter.10
  245.1 44.2 all-gather.9
  293.3 71.4 reduce-scatter.6
  367.6 42.5 reduce-scatter.8
where the time goes:
time: 421 us
  waiting for transfers between devices  243 us (58%)
  blocking collectives  85.3 us (20%)
  matrix products  40.2 us (10%)
  local copies, waits for them, and re-layouts  16.1 us (4%)
  between operations  14.2 us (3%)
  other arithmetic  11.5 us (3%)
  starting transfers between devices  6.02 us (1%)
  loops' own time  4.31 us (1%)
    reduce_scatter x1, waiting for transfers between devices, per_device(): lax.psum_scatter(jnp.einsum('mch,mth->ct', rows_block, grads, preferred_e...  67 us
    all_gather x1, waiting for transfers between devices, per_device(): lax.all_gather(normed, ('gx', 'gy'), axis=1, tiled=True)  55.2 us
    all_gather x1, waiting for transfers between devices, per_device(): segment = lax.all_gather(grad_out, ('gx', 'gy'), axis=1, tiled=True)  47.6 us
    psum x1, blocking collectives, per_device(): squares = lax.psum(jnp.sum(inputs_f * inputs_f, axis=1), ('gx', 'gy'))  35.2 us
    psum x1, blocking collectives, per_device(): norm_dots = lax.psum(jnp.sum(upstream * scaled, axis=1), ('gx', 'gy'))  30.5 us
    all_to_all x1, waiting for transfers between devices, per_device(): lax.all_to_all(wo_full, ('gx', 'gy'), split_axis=1, concat_axis=0, tiled=...  25.8 us
    all_gather x1, waiting for transfers between devices, per_device(): all_heads = lax.all_gather(attended, ('gx', 'gy'), axis=1, tiled=True)  19.1 us
    all_gather x1, blocking collectives, per_device(): lax.all_gather(jnp.concatenate([projected[1], projected[2]], axis=1), 'gz...  13.9 us
  transfers between devices with their start and end apart: 10, of which 9 were waited for; matrix products, arithmetic and copies ran while one was open for 11% of the time, Pallas kernels for 0%

commit v1 on v0

--- a/solution.py
+++ b/solution.py
@@ -190,7 +190,9 @@
         .T
     )
     upstream = grad_normed * row_gain
-    norm_dots = lax.psum(jnp.sum(upstream * scaled, axis=1), ("gx", "gy"))
+    norm_dots = jnp.sum(upstream * scaled, axis=1)
+    for mesh_axis in ("gx", "gy"):
+        norm_dots = lax.psum(norm_dots, mesh_axis)
     grad_in = (inv_rms[:, None] * (upstream - scaled * (norm_dots / full_width)[:, None])).astype(
         jnp.bfloat16
     )

time: 421 us -> 422 us (level)
  blocking collectives: 85.3 us -> 71.1 us
  waiting for transfers between devices: 243 us -> 257 us
    psum x1 -> x2, blocking collectives: 30.5 us -> 16.3 us  [per_device(): norm_dots = lax.psum(norm_dots, mesh_axis)]
    reduce_scatter x1, waiting for transfers between devices: 6.36 us -> 20.6 us  [per_device(): lax.psum_scatter(w_grad.astype(jnp.bfloat16), 'gz', scatter_dimension=1,...]
where the time goes in v1:
time: 422 us; the launch traced here: 421 us
  waiting for transfers between devices  257 us (61%)
  blocking collectives  71.1 us (17%)
  matrix products  40.1 us (10%)
  local copies, waits for them, and re-layouts  16.1 us (4%)
  between operations  14.2 us (3%)
  other arithmetic  11.5 us (3%)
  starting transfers between devices  6.02 us (1%)
  loops' own time  4.31 us (1%)
    reduce_scatter x1, waiting for transfers between devices, per_device(): lax.psum_scatter(jnp.einsum('mch,mth->ct', rows_block, grads, preferred_e...  67 us
    all_gather x1, waiting for transfers between devices, per_device(): lax.all_gather(normed, ('gx', 'gy'), axis=1, tiled=True)  55.2 us
    all_gather x1, waiting for transfers between devices, per_device(): segment = lax.all_gather(grad_out, ('gx', 'gy'), axis=1, tiled=True)  47.6 us
    psum x1, blocking collectives, per_device(): squares = lax.psum(jnp.sum(inputs_f * inputs_f, axis=1), ('gx', 'gy'))  35.2 us
    all_to_all x1, waiting for transfers between devices, per_device(): lax.all_to_all(wo_full, ('gx', 'gy'), split_axis=1, concat_axis=0, tiled=...  25.8 us
    reduce_scatter x1, waiting for transfers between devices, per_device(): lax.psum_scatter(w_grad.astype(jnp.bfloat16), 'gz', scatter_dimension=1,...  20.6 us
    all_gather x1, waiting for transfers between devices, per_device(): all_heads = lax.all_gather(attended, ('gx', 'gy'), axis=1, tiled=True)  19.1 us
    psum x2, blocking collectives, per_device(): norm_dots = lax.psum(norm_dots, mesh_axis)  16.3 us
  transfers between devices with their start and end apart: 10, of which 9 were waited for; matrix products, arithmetic and copies ran while one was open for 11% of the time, Pallas kernels for 0%

profile of v1, /device:TPU:0, one launch (start us, length us, event | category | flops | bytes accessed | tf_op | source)
XLA Modules:
  0.0 420.7 jit_solution(16494984096274325145)
XLA Ops:
  7.3 2.7 copy.44
  10.2 35.2 %psum.28 = f32[512]{0:T(512)S(1)} all-reduce(f32[512]{0:T(512)S(1)} %fusion.65), channel_id=1, replica_groups=mesh['gx'=4,'gy'=4,'gz'=2] {'gx','gy'}, use_global_device_ids=true, to_apply=%region_1.0 | all-reduce | flops 512 | bytes 4096 | tf_op jit(solution)/shard_map/psum | solution.py:30
  45.4 0.9 fusion.66
  46.4 1.0 copy.50
  48.3 9.6 %all-gather.8.cloned.1.call-done = bf16[3,4096,128]{1,2,0:T(8,128)(2,1)} async-done(((bf16[3,2048,128]{1,2,0:T(8,128)(2,1)}), bf16[3,4096,128]{1,2,0:T(8,128)(2,1)}) %all-gather.8.cloned.1.call-update) | async-done | bytes 3145744 | tf_op jit(solution)/shard_map/all_gather | solution.py:35
  57.8 55.2 %all-gather.6.cloned.1.call-done = bf16[512,4096]{1,0:T(8,128)(2,1)} async-done(((bf16[512,256]{1,0:T(8,128)(2,1)}), bf16[512,4096]{1,0:T(8,128)(2,1)}) %all-gather.6.cloned.1.call-update) | async-done | bytes 4194320 | tf_op jit(solution)/shard_map/all_gather | solution.py:40
  113.0 5.0 %fusion.75 = f32[512,384]{0,1:S(1)} fusion(bf16[512,4096]{1,0:T(8,128)(2,1)} %all-gather.6.cloned.1.call-done, bf16[4096,384]{0,1:T(8,128)(2,1)} %bitcast.156), kind=kOutput, calls=%fused_computation.134 | convolution fusion | flops 1610612736 | bytes 8126464
  118.1 13.9 %all_gather.21 = bf16[1024,256]{0,1:T(8,128)(2,1)S(1)} all-gather(bf16[512,256]{0,1:T(8,128)(2,1)S(1)} %pad_maximum_fusion.1), channel_id=1, replica_groups=mesh['gx'=4,'gy'=4,'gz'=2] {'gz'}, dimensions={0}, use_global_device_ids=true | all-gather | bytes 786432 | tf_op jit(solution)/shard_map/all_gather | solution.py:46
  132.4 4.8 %while.43 = (s32[]{:T(128)}, f32[512]{0:T(512)S(1)}, f32[512]{0:T(512)S(1)}, s32[2]{0:T(128)S(1)}, s32[512]{0:T(512)S(1)}, /*index=5*/s32[2,8]{1,0:T(2,128)S(1)}...) while((s32[]{:T(128)}, f32[512]{0:T(512)S(1)}, ...), condition=%wide.region_7.8_spmd.clone, body=%wide.region_3.7_spmd.clone.sunk | while | flops 70803472 | bytes 2418638 | solution.py:84
  132.4 0.6 dynamic_slice.46
  134.8 0.6 dynamic_slice.46
  137.2 0.6 log_add_fusion
  137.8 5.9 %while.44 = (s32[]{:T(128)}, f32[512,128]{1,0:T(8,128)S(1)}, s32[2]{0:T(128)S(1)}, s32[512]{0:T(512)S(1)}, s32[2,8]{1,0:T(2,128)S(1)}, /*index=5*/bf16[1024,256]...) while((s32[]{:T(128)}, f32[512,128]{1,0:T(8,128)S(1)}, ...), condition=%wide.region_10.11_spmd.clone, body=%wide.region_8.10_spmd.clone.sunk | while | flops 136467984 | bytes 945628 | solution.py:103
  137.8 0.6 dynamic_slice.47
  139.1 1.5 fusion.118
  140.7 0.6 dynamic_slice.47
  142.1 1.5 fusion.118
  143.8 47.6 %all-gather.14.cloned.1.call-done = bf16[512,4096]{1,0:T(8,128)(2,1)} async-done(((bf16[512,256]{1,0:T(8,128)(2,1)}), bf16[512,4096]{1,0:T(8,128)(2,1)}) %all-gather.14.cloned.1.call-update) | async-done | bytes 4194320 | tf_op jit(solution)/shard_map/all_gather | solution.py:116
  191.3 4.0 multiply_reduce_fusion
  196.0 9.3 %while.45 = (s32[]{:T(128)}, f32[512,128]{1,0:T(8,128)S(1)}, bf16[2,512,256]{1,2,0:T(8,128)(2,1)S(1)}, s32[2]{0:T(128)}, s32[512]{0:T(512)S(1)}, /*index=5*/s32[...) while((s32[]{:T(128)}, f32[512,128]{1,0:T(8,128)S(1)}, ...), condition=%wide.region_15.16_spmd.clone, body=%wide.region_13.15_spmd.clone.sunk | while | flops 339367424 | bytes 6974985 | solution.py:149
  196.0 1.2 dynamic_slice.48
  198.0 1.2 fusion.129
  200.6 1.2 dynamic_slice.48
  202.7 1.2 fusion.129
  205.3 1.0 copy.56
  206.4 3.9 convolution_convert_fusion.1
  210.3 0.7 all-gather.10.cloned.1.call-update
  211.1 8.2 %reduce-scatter.5.cloned.1.call-done = bf16[512,256]{1,0:T(8,128)(2,1)} async-done(((bf16[1024,256]{1,0:T(8,128)(2,1)}), bf16[512,256]{1,0:T(8,128)(2,1)}) %reduce-scatter.5.cloned.1.call-update) | async-done | bytes 262160 | tf_op jit(solution)/shard_map/reduce_scatter | solution.py:152
  219.3 1.0 slice_bitcast_fusion.7
  220.2 5.8 %fusion.52 = bf16[4096,512]{0,1:T(8,128)(2,1)} fusion(bf16[3,4096,128]{1,2,0:T(8,128)(2,1)} %all-gather.8.cloned.1.call-done, bf16[1,512,128]{2,1,0:T(8,128)(2,1)S(1)} %get-tuple-element.678, bf16[1,512,128]{2,1,0:T(8,128)(2,1)S(1)} %get-tuple-element.677, bf16[1,512,128]{2,1,0:T(8,128)(2,1)S(1)} %convert_bitcast_fusion.1), kind=kOutput, calls=%fused_computation.84 | convolution fusion | flops 1613103104 | bytes 7733248 | tf_op jit(solution)/shard_map/mch,mth->ct/dot_general | solution.py:182
  226.3 6.1 %fusion.53 = bf16[3,4096,128]{1,2,0:T(8,128)(2,1)} fusion(bf16[512,4096]{1,0:T(8,128)(2,1)} %all-gather.6.cloned.1.call-done, bf16[1,512,128]{2,1,0:T(8,128)(2,1)S(1)} %get-tuple-element.678, bf16[1,512,128]{2,1,0:T(8,128)(2,1)S(1)} %get-tuple-element.677, bf16[1,512,128]{2,1,0:T(8,128)(2,1)S(1)} %convert_bitcast_fusion.1), kind=kOutput, calls=%fused_computation.85 | convolution fusion | flops 1612578816 | bytes 7733248 | tf_op jit(solution)/shard_map/tc,mth->mch/dot_general | solution.py:165
  232.4 1.3 copy.51
  233.8 5.5 %all-to-all-start = ((bf16[128,16,256]{2,0,1:T(8,128)(2,1)}), bf16[128,16,256]{2,0,1:T(8,128)(2,1)S(1)}, u32[]{:S(2)}, u32[]{:S(2)}) async-start(bf16[128,16,256]{2,0,1:T(8,128)(2,1)} %copy.51), calls=%async_computation | async-start | bytes 2097152 | tf_op jit(solution)/shard_map/all_to_all | solution.py:106
  239.3 3.1 reduce-scatter.11.cloned.1.call-done
  242.4 2.1 convert_element_type.104
  244.5 25.8 %all-to-all-done = bf16[128,16,256]{2,0,1:T(8,128)(2,1)S(1)} async-done(((bf16[128,16,256]{2,0,1:T(8,128)(2,1)}), bf16[128,16,256]{2,0,1:T(8,128)(2,1)S(1)}, u32[]{:S(2)}, u32[]{:S(2)}) %all-to-all-start) | async-done | bytes 1048608 | tf_op jit(solution)/shard_map/all_to_all | solution.py:106
  270.3 19.1 %all-gather.10.cloned.1.call-done = bf16[512,2048]{0,1:T(8,128)(2,1)} async-done(((bf16[512,128]{0,1:T(8,128)(2,1)}), bf16[512,2048]{0,1:T(8,128)(2,1)}) %all-gather.10.cloned.1.call-update) | async-done | bytes 2097168 | tf_op jit(solution)/shard_map/all_gather | solution.py:105
  289.4 4.8 %convolution_convert_fusion.2 = bf16[16,512,256]{2,1,0:T(8,128)(2,1)} fusion(bf16[512,16,128]{0,2,1:T(8,128)(2,1)} %bitcast.147, bf16[128,16,256]{2,0,1:T(8,128)(2,1)S(1)} %all-to-all-done), kind=kOutput, calls=%fused_computation.88 | convolution fusion | flops 538968064 | bytes 7340032 | tf_op jit(solution)/shard_map/thd,hdc->htc/dot_general | solution.py:108
  294.2 3.5 reduce_sum.98
  297.8 67.0 %reduce-scatter.7.cloned.1.call-done = bf16[256,512]{0,1:T(8,128)(2,1)} async-done(((bf16[4096,512]{0,1:T(8,128)(2,1)}), bf16[256,512]{0,1:T(8,128)(2,1)}) %reduce-scatter.7.cloned.1.call-update) | async-done | bytes 262160 | tf_op jit(solution)/shard_map/reduce_scatter | solution.py:181
  364.8 1.3 fusion.59
  366.1 5.9 %psum.29 = f32[512]{0:T(512)S(1)} all-reduce(f32[512]{0:T(512)S(1)} %fusion.59), channel_id=1, replica_groups=mesh['gx'=4,'gy'=4,'gz'=2] {'gx'}, use_global_device_ids=true, to_apply=%region_19.20 | all-reduce | flops 512 | bytes 4096 | tf_op jit(solution)/shard_map/psum | solution.py:195
  372.0 10.5 %psum.30 = f32[512]{0:T(512)S(1)} all-reduce(f32[512]{0:T(512)S(1)} %psum.29), channel_id=1, replica_groups=mesh['gx'=4,'gy'=4,'gz'=2] {'gy'}, use_global_device_ids=true, to_apply=%region_20.21 | all-reduce | flops 512 | bytes 4096 | tf_op jit(solution)/shard_map/psum | solution.py:195
  382.4 1.5 fusion.63
  383.9 5.7 %psum.31 = f32[2,256]{1,0:T(2,128)} all-reduce(f32[2,256]{1,0:T(2,128)S(1)} %fusion.63), channel_id=1, replica_groups=mesh['gx'=4,'gy'=4,'gz'=2] {'gz'}, use_global_device_ids=true, to_apply=%region_23.24 | all-reduce | flops 512 | bytes 4096 | tf_op jit(solution)/shard_map/psum | solution.py:201
  389.6 20.6 %reduce-scatter.9.cloned.1.call-done = bf16[3,2048,128]{1,2,0:T(8,128)(2,1)} async-done(((bf16[3,4096,128]{1,2,0:T(8,128)(2,1)}), bf16[3,2048,128]{1,2,0:T(8,128)(2,1)}) %reduce-scatter.9.cloned.1.call-update) | async-done | bytes 1572880 | tf_op jit(solution)/shard_map/reduce_scatter | solution.py:172
  410.2 3.1 copy.59
  413.2 1.0 fusion.62
  (130 shorter events, 8.0 us)
Async XLA Ops:
  7.2 2.8 copy-start
  7.2 38.2 %copy-start.12 = (s32[512]{0:T(512)S(1)}, s32[512]{0:T(512)}, u32[]{:S(2)}) copy-start(s32[512]{0:T(512)} %param.14) | copy-start | bytes 6148
  7.2 38.2 %copy-start.14 = (f32[2,256]{1,0:T(2,128)S(1)}, f32[2,256]{1,0:T(2,128)}, u32[]{:S(2)}) copy-start(f32[2,256]{1,0:T(2,128)} %param.16) | copy-start | bytes 6148
  7.2 39.2 %copy-start.4 = (bf16[128,2048]{1,0:T(8,128)(2,1)S(1)}, bf16[128,2048]{1,0:T(8,128)(2,1)}, u32[]{:S(2)}) copy-start(bf16[128,2048]{1,0:T(8,128)(2,1)} %param.18) | copy-start | bytes 1572868
  7.2 40.9 %copy-start.5 = (s32[2,8]{1,0:T(2,128)S(1)}, s32[2,8]{1,0:T(2,128)}, u32[]{:S(2)}) copy-start(s32[2,8]{1,0:T(2,128)} %param.15) | copy-start | bytes 196
  7.2 50.6 %all-gather.8.cloned.1.call-start = ((), (), s32[]{:S(2)}) async-start(), calls=%async_computation.6 | async-start | bytes 4718592 | tf_op jit(solution)/shard_map/all_gather | solution.py:35
  10.0 103.0 %all-gather.6.cloned.1.call-start = ((), (), s32[]{:S(2)}) async-start(), calls=%async_computation.5 | async-start | bytes 4456448 | tf_op jit(solution)/shard_map/all_gather | solution.py:40
  45.4 67.6 %copy-start.10 = (pred[512]{0:T(512)(128)(4,1)}, pred[512]{0:T(512)(128)(4,1)S(1)}, u32[]{:S(2)}) copy-start(pred[512]{0:T(512)(128)(4,1)S(1)} %broadcast_compare_fusion.3) | copy-start | bytes 1540
  45.4 67.6 %copy-start.8 = (f32[1,256]{1,0:T(1,128)}, f32[1,256]{1,0:T(1,128)S(1)}, u32[]{:S(2)}) copy-start(f32[1,256]{1,0:T(1,128)S(1)} %get-tuple-element.680) | copy-start | bytes 3076
  45.4 72.6 %copy-start.6 = (f32[1,256]{1,0:T(1,128)}, f32[1,256]{1,0:T(1,128)S(1)}, u32[]{:S(2)}) copy-start(f32[1,256]{1,0:T(1,128)S(1)} %get-tuple-element.679) | copy-start | bytes 3076
  46.3 97.4 %all-gather.12.cloned.1.call-start = ((), (), s32[]{:S(2)}) async-start(), calls=%async_computation.8 | async-start | bytes 1572864 | tf_op jit(solution)/shard_map/all_gather | solution.py:36
  47.4 143.9 %all-gather.14.cloned.1.call-start = ((), (), s32[]{:S(2)}) async-start(), calls=%async_computation.9 | async-start | bytes 4456448 | tf_op jit(solution)/shard_map/all_gather | solution.py:116
  48.0 171.2 %reduce-scatter.5.cloned.1.call-start = ((), (), s32[]{:S(2)}) async-start(), calls=%async_computation.10 | async-start | bytes 786432 | tf_op jit(solution)/shard_map/reduce_scatter | solution.py:152
  143.7 62.6 %copy-start.2 = (bf16[512,128]{0,1:T(8,128)(2,1)}, bf16[512,128]{0,1:T(8,128)(2,1)S(1)}, u32[]{:S(2)}) copy-start(bf16[512,128]{0,1:T(8,128)(2,1)S(1)} %copy.49) | copy-start | bytes 393220
  206.3 36.1 %reduce-scatter.11.cloned.1.call-start = ((), (), s32[]{:S(2)}) async-start(), calls=%async_computation.13 | async-start | bytes 1572864 | tf_op jit(solution)/shard_map/reduce_scatter | solution.py:175
  210.3 79.1 %all-gather.10.cloned.1.call-start = ((), (), s32[]{:S(2)}) async-start(), calls=%async_computation.7 | async-start | bytes 2228224 | tf_op jit(solution)/shard_map/all_gather | solution.py:105
  211.0 153.7 %reduce-scatter.7.cloned.1.call-start = ((), (), s32[]{:S(2)}) async-start(), calls=%async_computation.11 | async-start | bytes 4456448 | tf_op jit(solution)/shard_map/reduce_scatter | solution.py:181
  226.1 6.4 %copy-start.1 = (bf16[128,4096]{0,1:T(8,128)(2,1)S(1)}, bf16[128,4096]{0,1:T(8,128)(2,1)}, u32[]{:S(2)}) copy-start(bf16[128,4096]{0,1:T(8,128)(2,1)} %all-gather.12.cloned.1.call-done) | copy-start | bytes 3145732
  226.1 184.1 %reduce-scatter.9.cloned.1.call-start = ((), (), s32[]{:S(2)}) async-start(), calls=%async_computation.12 | async-start | bytes 4718592 | tf_op jit(solution)/shard_map/reduce_scatter | solution.py:172
  233.8 36.5 %all-to-all-start = ((bf16[128,16,256]{2,0,1:T(8,128)(2,1)}), bf16[128,16,256]{2,0,1:T(8,128)(2,1)S(1)}, u32[]{:S(2)}, u32[]{:S(2)}) async-start(bf16[128,16,256]{2,0,1:T(8,128)(2,1)} %copy.51), calls=%async_computation | async-start | bytes 2097152 | tf_op jit(solution)/shard_map/all_to_all | solution.py:106
  289.4 75.4 %copy-start.7 = (f32[1,256]{1,0:T(1,128)S(1)}, f32[1,256]{1,0:T(1,128)}, u32[]{:S(2)}) copy-start(f32[1,256]{1,0:T(1,128)} %copy-done.6) | copy-start | bytes 3076
  289.4 75.4 %copy-start.9 = (f32[1,256]{1,0:T(1,128)S(1)}, f32[1,256]{1,0:T(1,128)}, u32[]{:S(2)}) copy-start(f32[1,256]{1,0:T(1,128)} %copy-done.8) | copy-start | bytes 3076
  289.4 75.4 %copy-start.11 = (pred[512]{0:T(512)(128)(4,1)S(1)}, pred[512]{0:T(512)(128)(4,1)}, u32[]{:S(2)}) copy-start(pred[512]{0:T(512)(128)(4,1)} %copy-done.10) | copy-start | bytes 1540
  294.2 88.2 %copy-start.13 = (s32[512]{0:T(512)S(1)}, s32[512]{0:T(512)}, u32[]{:S(2)}) copy-start(s32[512]{0:T(512)} %param.14) | copy-start | bytes 6148
  364.8 48.5 %copy-start.3 = (bf16[256,512]{0,1:T(8,128)(2,1)S(1)}, bf16[256,512]{0,1:T(8,128)(2,1)}, u32[]{:S(2)}) copy-start(bf16[256,512]{0,1:T(8,128)(2,1)} %reduce-scatter.7.cloned.1.call-done) | copy-start | bytes 786436
Sparse Core Ops, SparseCore 0:
  10.1 47.6 all-gather.7
  60.5 52.4 all-gather.5
  115.1 23.5 all-gather.11
  140.6 50.6 all-gather.13
  206.4 12.7 reduce-scatter.4
  221.9 20.3 reduce-scatter.10
  245.2 44.2 all-gather.9
  293.3 71.4 reduce-scatter.6
  367.6 42.5 reduce-scatter.8
